TPU v7x, 32 devices: a whole 2x2x4 slice. The times are simulated.
32 devices in a mesh: batch: 2 (over core), neuron: 16 (over z, y, x).
Axes of the slice: x: 2, y: 2, z: 4, core: 2. Of those that a mesh axis runs over, the one named last changes fastest.
Arguments:
- images: bfloat16 [32, 65536], P('batch', 'neuron'), parts along dimension 0, may hold values from 0 to 32
- tile_weights: bfloat16 [2, 2048, 128, 128], P(None, 'neuron'), may hold values from -0.375 to 0.375
- tile_blocks: int32 [2, 2048, 2], P(None, 'neuron'), may hold values from 0 to 511, as said below
- tile_count: int32 [2, 16], P(None, 'neuron'), may hold values from 96 to 128, as said below
- bias: float32 [2, 65536], P(None, 'neuron'), may hold values from -48 to 48
Outputs:
- activity: bfloat16 [32, 65536], P('batch', 'neuron'), parts along dimension 0
There are 2 independent parts, one for each index of `batch`. A program takes and returns all parts, laid end to end along the dimension named above; an argument that names none is the same for every part. Nothing has to cross between parts.
Inputs may be any that keep to these rules, and one draw needn't show every extreme that they name: Slots 0 to tile_count[l, d] - 1 of device d are live in layer l; in every layer one device has all 128 live. `tile_blocks`: entry [l, d * 128 + s, :] is the row block and column block of slot s of device d. Within one device and layer the column blocks are all different, and at most 8 of them lie among the 32 column blocks of any one neuron device; in every layer the column blocks of some neuron device get exactly 8 live slots from every device.
All inputs are finite; a program needn't handle non-finite values.
Results may differ from a plain program's by a relative error of at most 0.0033.
Values may be sent and summed in bfloat16 or wider, within the bound.
A program may use at most 64 MiB of HBM per device.

v0:
```python
import jax
import jax.numpy as jnp
from jax import lax
from jax.sharding import PartitionSpec as P

CEILING = 32.0


def local(images, tile_weights, tile_blocks, tile_count, bias):
    devices = lax.axis_size("neuron")
    layer_total = tile_weights.shape[0]
    slot_total = tile_weights.shape[1]
    block_width = tile_weights.shape[2]
    image_rows, local_width = images.shape
    own_blocks = local_width // block_width
    all_blocks = own_blocks * devices
    capacity = max(2, slot_total // devices)
    slot_ids = jnp.arange(slot_total, dtype=jnp.int32)
    activity = images
    for layer_index in range(layer_total):
        whole_acts = lax.all_gather(activity, "neuron", axis=1, tiled=True)
        block_view = whole_acts.reshape(image_rows, all_blocks, block_width)
        row_ids = tile_blocks[layer_index, :, 0]
        col_ids = tile_blocks[layer_index, :, 1]
        usable = slot_ids < tile_count[layer_index, 0]
        picked = jnp.take(block_view, row_ids, axis=1)
        products = jnp.einsum(
            "bsk,skn->sbn", picked, tile_weights[layer_index], preferred_element_type=jnp.float32
        )
        products = jnp.where(usable[:, None, None], products, 0.0)
        owners = col_ids // own_blocks
        local_block = (col_ids % own_blocks).astype(jnp.float32)
        same_owner = (
            (owners[:, None] == owners[None, :])
            & usable[None, :]
            & (slot_ids[None, :] < slot_ids[:, None])
        )
        slot_rank = jnp.sum(same_owner.astype(jnp.int32), axis=1)
        targets = jnp.where(usable, owners * capacity + slot_rank, devices * capacity)
        outgoing = (
            jnp.zeros((devices * capacity, image_rows, block_width), jnp.float32)
            .at[targets]
            .set(products, mode="drop")
        )
        labels = (
            jnp.full((devices * capacity,), -1.0, jnp.float32)
            .at[targets]
            .set(local_block, mode="drop")
        )
        incoming, arrived_ids = (
            lax.all_to_all(outgoing, "neuron", split_axis=0, concat_axis=0, tiled=True),
            lax.all_to_all(labels, "neuron", split_axis=0, concat_axis=0, tiled=True),
        )
        selector = (
            arrived_ids[None, :] == jnp.arange(own_blocks, dtype=jnp.float32)[:, None]
        ).astype(jnp.float32)
        summed = jnp.einsum("or,rbn->obn", selector, incoming, precision=lax.Precision.HIGHEST)
        summed = jnp.transpose(summed, (1, 0, 2)).reshape(image_rows, local_width)
        activity = jnp.clip(summed + bias[layer_index][None, :], 0.0, CEILING).astype(jnp.bfloat16)
    return activity


def solution(mesh):
    in_specs = (
        P("batch", "neuron"),
        P(None, "neuron", None, None),
        P(None, "neuron", None),
        P(None, "neuron"),
        P(None, "neuron"),
    )
    out_specs = P("batch", "neuron")
    return jax.shard_map(local, mesh=mesh, in_specs=in_specs, out_specs=out_specs, check_vma=False)
```

profile of v0, /device:TPU:8, one launch (start us, length us, event | category | flops | bytes accessed | tf_op | source)
XLA Modules:
  0.0 240.6 jit_solution(3494090513267543889)
XLA Ops:
  6.5 0.0 all-gather.3.cloned.1.call-start
  6.5 0.7 all-gather.3.cloned.1.call-update
  7.3 1.3 fusion.47
  8.5 0.6 iota_compare_fusion.3
  9.2 0.6 iota_compare_fusion.4
  9.8 0.7 fusion.37
  10.4 0.7 fusion.36
  11.2 0.7 and_select_fusion.4
  11.8 0.2 convert_reduce_fusion
  12.0 1.9 fusion.39
  13.9 1.0 scatter_custom_fusion.1
  14.9 0.7 all_to_all.20
  15.6 7.2 %all-to-all-start.1 = ((f32[16,8,1]{1,2,0:T(1,128)}), f32[16,8,1]{1,2,0:T(1,128)S(1)}, u32[]{:S(2)}, u32[]{:S(2)}) async-start(f32[16,8,1]{1,2,0:T(1,128)} %bitcast.13), calls=%async_computation.1 | async-start | bytes 16384 | tf_op jit(solution)/shard_map/all_to_all | solution.py:52
  22.8 0.7 compare_and_fusion
  23.5 48.0 %all-gather.3.cloned.1.call-done = bf16[16,65536]{1,0:T(8,128)(2,1)} async-done(((bf16[16,4096]{1,0:T(8,128)(2,1)}), bf16[16,65536]{1,0:T(8,128)(2,1)}) %all-gather.3.cloned.1.call-update) | async-done | bytes 2097168 | tf_op jit(solution)/shard_map/all_gather | solution.py:21
  71.6 2.0 copy_bitcast_fusion.1
  73.5 0.7 gather_fusion
  74.2 3.2 %fusion.6 = f32[128,16,128]{2,1,0:T(8,128)S(1)} fusion(bf16[2,128,128,128]{3,2,1,0:T(8,128)(2,1)} %param.8, bf16[128,16,128]{2,1,0:T(8,128)(2,1)S(1)} %gather_fusion, pred[128]{0:T(512)(128)(4,1)S(1)} %get-tuple-element.16, pred[128]{0:T(512)(128)(4,1)S(1)} %iota_compare_fusion.3), kind=kOutput, calls=%fused_computation.14 | convolution fusion | flops 67633152 | bytes 5767424 | tf_op jit(solution)/shard_map/bsk,skn->sbn/dot_general | solution.py:27
  77.4 1.0 broadcast.299.clone
  78.5 0.0 copy-start
  78.5 13.5 %scatter_fusion = f32[128,16,128]{2,1,0:T(8,128)} fusion(f32[128,16,128]{2,1,0:T(8,128)} %broadcast.299.clone, s32[128]{0:T(128)S(1)} %get-tuple-element.18, f32[128,16,128]{2,1,0:T(8,128)S(1)} %fusion.6), kind=kCustom, calls=%fused_computation.4 | custom fusion | bytes 3146240 | tf_op jit(solution)/shard_map/scatter | solution.py:43
  91.9 0.0 all-to-all-done.1
  91.9 5.2 %all-to-all-start.2 = ((f32[128,16,128]{2,1,0:T(8,128)}), f32[128,16,128]{2,1,0:T(8,128)S(1)}, u32[]{:S(2)}, u32[]{:S(2)}) async-start(f32[128,16,128]{2,1,0:T(8,128)} %scatter_fusion), calls=%async_computation.2 | async-start | bytes 2097152 | tf_op jit(solution)/shard_map/all_to_all | solution.py:51
  97.1 0.0 all-gather.5.cloned.1.call-start
  97.2 0.0 copy-done
  97.2 0.6 broadcast.370
  97.8 0.6 reduce.6
  98.4 0.1 eq.69
  98.5 23.1 %all-to-all-done.2 = f32[128,16,128]{2,1,0:T(8,128)S(1)} async-done(((f32[128,16,128]{2,1,0:T(8,128)}), f32[128,16,128]{2,1,0:T(8,128)S(1)}, u32[]{:S(2)}, u32[]{:S(2)}) %all-to-all-start.2) | async-done | bytes 1048608 | tf_op jit(solution)/shard_map/all_to_all | solution.py:51
  121.6 0.7 fusion.14
  122.3 0.8 fusion.25
  123.2 0.0 all-gather.5.cloned.1.call-update
  123.2 1.0 scatter_custom_fusion
  124.2 0.7 all_to_all.18
  124.8 4.7 %all-to-all-start = ((f32[16,8,1]{1,2,0:T(1,128)}), f32[16,8,1]{1,2,0:T(1,128)S(1)}, u32[]{:S(2)}, u32[]{:S(2)}) async-start(f32[16,8,1]{1,2,0:T(1,128)} %bitcast.5), calls=%async_computation | async-start | bytes 16384 | tf_op jit(solution)/shard_map/all_to_all | solution.py:52
  129.6 52.7 %all-gather.5.cloned.1.call-done = bf16[16,65536]{1,0:T(8,128)(2,1)} async-done(((bf16[16,4096]{1,0:T(8,128)(2,1)}), bf16[16,65536]{1,0:T(8,128)(2,1)}) %all-gather.5.cloned.1.call-update) | async-done | bytes 2097168 | tf_op jit(solution)/shard_map/all_gather | solution.py:21
  182.3 2.0 copy_bitcast_fusion
  184.2 0.7 gather_fusion.1
  184.9 3.2 %fusion.9 = f32[128,16,128]{2,1,0:T(8,128)S(1)} fusion(bf16[2,128,128,128]{3,2,1,0:T(8,128)(2,1)} %param.8, bf16[128,16,128]{2,1,0:T(8,128)(2,1)S(1)} %gather_fusion.1, pred[128]{0:T(512)(128)(4,1)S(1)} %get-tuple-element.8, pred[128]{0:T(512)(128)(4,1)S(1)} %iota_compare_fusion.4), kind=kOutput, calls=%fused_computation.15 | convolution fusion | flops 67633152 | bytes 5767424 | tf_op jit(solution)/shard_map/bsk,skn->sbn/dot_general | solution.py:27
  188.1 1.0 broadcast.299
  189.2 13.4 %scatter_fusion.1 = f32[128,16,128]{2,1,0:T(8,128)} fusion(f32[128,16,128]{2,1,0:T(8,128)} %broadcast.299, s32[128]{0:T(128)S(1)} %get-tuple-element.19, f32[128,16,128]{2,1,0:T(8,128)S(1)} %fusion.9), kind=kCustom, calls=%fused_computation.5 | custom fusion | bytes 3146240 | tf_op jit(solution)/shard_map/scatter | solution.py:43
  202.5 0.0 all-to-all-done
  202.5 5.2 %all-to-all-start.3 = ((f32[128,16,128]{2,1,0:T(8,128)}), f32[128,16,128]{2,1,0:T(8,128)S(1)}, u32[]{:S(2)}, u32[]{:S(2)}) async-start(f32[128,16,128]{2,1,0:T(8,128)} %scatter_fusion.1), calls=%async_computation.3 | async-start | bytes 2097152 | tf_op jit(solution)/shard_map/all_to_all | solution.py:51
  207.8 0.6 reduce.7
  208.4 0.1 eq.62
  208.5 23.7 %all-to-all-done.3 = f32[128,16,128]{2,1,0:T(8,128)S(1)} async-done(((f32[128,16,128]{2,1,0:T(8,128)}), f32[128,16,128]{2,1,0:T(8,128)S(1)}, u32[]{:S(2)}, u32[]{:S(2)}) %all-to-all-start.3) | async-done | bytes 1048608 | tf_op jit(solution)/shard_map/all_to_all | solution.py:51
  232.2 0.7 fusion.12
  233.0 0.8 fusion.23
  (3 shorter events, 0.0 us)
Async XLA Ops:
  6.5 65.0 %all-gather.3.cloned.1.call-start = ((), (), s32[]{:S(2)}) async-start(), calls=%async_computation.4 | async-start | bytes 2228224 | tf_op jit(solution)/shard_map/all_gather | solution.py:21
  15.6 76.3 %all-to-all-start.1 = ((f32[16,8,1]{1,2,0:T(1,128)}), f32[16,8,1]{1,2,0:T(1,128)S(1)}, u32[]{:S(2)}, u32[]{:S(2)}) async-start(f32[16,8,1]{1,2,0:T(1,128)} %bitcast.13), calls=%async_computation.1 | async-start | bytes 16384 | tf_op jit(solution)/shard_map/all_to_all | solution.py:52
  78.5 18.7 %copy-start = (f32[2,4096]{1,0:T(2,128)S(1)}, f32[2,4096]{1,0:T(2,128)}, u32[]{:S(2)}) copy-start(f32[2,4096]{1,0:T(2,128)} %param.11) | copy-start | bytes 98308
  91.9 29.6 %all-to-all-start.2 = ((f32[128,16,128]{2,1,0:T(8,128)}), f32[128,16,128]{2,1,0:T(8,128)S(1)}, u32[]{:S(2)}, u32[]{:S(2)}) async-start(f32[128,16,128]{2,1,0:T(8,128)} %scatter_fusion), calls=%async_computation.2 | async-start | bytes 2097152 | tf_op jit(solution)/shard_map/all_to_all | solution.py:51
  97.1 85.2 %all-gather.5.cloned.1.call-start = ((), (), s32[]{:S(2)}) async-start(), calls=%async_computation.5 | async-start | bytes 2228224 | tf_op jit(solution)/shard_map/all_gather | solution.py:21
  124.8 77.7 %all-to-all-start = ((f32[16,8,1]{1,2,0:T(1,128)}), f32[16,8,1]{1,2,0:T(1,128)S(1)}, u32[]{:S(2)}, u32[]{:S(2)}) async-start(f32[16,8,1]{1,2,0:T(1,128)} %bitcast.5), calls=%async_computation | async-start | bytes 16384 | tf_op jit(solution)/shard_map/all_to_all | solution.py:52
  202.5 29.7 %all-to-all-start.3 = ((f32[128,16,128]{2,1,0:T(8,128)}), f32[128,16,128]{2,1,0:T(8,128)S(1)}, u32[]{:S(2)}, u32[]{:S(2)}) async-start(f32[128,16,128]{2,1,0:T(8,128)} %scatter_fusion.1), calls=%async_computation.3 | async-start | bytes 2097152 | tf_op jit(solution)/shard_map/all_to_all | solution.py:51
Sparse Core Ops, SparseCore 0:
  10.1 61.4 all-gather.2
  123.3 58.9 all-gather.4
where the time goes:
time: 242 us; the launch traced here: 241 us
  waiting for transfers between devices  148 us (61%)
  local copies, waits for them, and re-layouts  39.6 us (16%)
  starting transfers between devices  22.4 us (9%)
  between operations  13.6 us (6%)
  other arithmetic  9.02 us (4%)
  matrix products  7.83 us (3%)
    all_gather x2, waiting for transfers between devices, local(): whole_acts = lax.all_gather(activity, 'neuron', axis=1, tiled=True)  101 us
    all_to_all x2, waiting for transfers between devices, local(): lax.all_to_all(outgoing, 'neuron', split_axis=0, concat_axis=0, tiled=True)  46.8 us
    scatter x2, local copies, waits for them, and re-layouts, local(): outgoing = jnp.zeros((devices * capacity, image_rows, block_width), jnp.f...  26.8 us
    all_to_all x2, starting transfers between devices, local(): lax.all_to_all(labels, 'neuron', split_axis=0, concat_axis=0, tiled=True)  12 us
    all_to_all x2, starting transfers between devices, local(): lax.all_to_all(outgoing, 'neuron', split_axis=0, concat_axis=0, tiled=True)  10.4 us
    dot_general x2, matrix products, local(): jnp.einsum('bsk,skn->sbn', picked, tile_weights[layer_index], preferred_e...  6.35 us
  transfers between devices with their start and end apart: 6, of which 4 were waited for; matrix products, arithmetic and copies ran while one was open for 22% of the time, Pallas kernels for 0%

commit v1 on v0

--- a/solution.py
+++ b/solution.py
@@ -18,7 +18,16 @@
     slot_ids = jnp.arange(slot_total, dtype=jnp.int32)
     activity = images
     for layer_index in range(layer_total):
-        whole_acts = lax.all_gather(activity, "neuron", axis=1, tiled=True)
+        ring = [activity]
+        for hop in range(15):
+            ring.append(
+                lax.ppermute(ring[-1], "neuron", [(dev, (dev + 1) % 16) for dev in range(16)])
+            )
+        whole_acts = jnp.roll(
+            jnp.concatenate(ring[::-1], axis=1),
+            (lax.axis_index("neuron") + 1) * ring[0].shape[1],
+            axis=1,
+        )
         block_view = whole_acts.reshape(image_rows, all_blocks, block_width)
         row_ids = tile_blocks[layer_index, :, 0]
         col_ids = tile_blocks[layer_index, :, 1]

time: 242 us -> 362 us (1.50)
  waiting for transfers between devices: 148 us -> 230 us
  starting transfers between devices: 22.4 us -> 66.2 us
  between operations: 13.6 us -> 0.48 us
  other arithmetic: 9.02 us -> 18.3 us
    ppermute x0 -> x30, waiting for transfers between devices: none -> 199 us  [local(): lax.ppermute(ring[-1], 'neuron', [(dev, (dev + 1) % 16) for dev in range(...]
    all_gather x2 -> x0, waiting for transfers between devices: 101 us -> none  [local(): whole_acts = lax.all_gather(activity, 'neuron', axis=1, tiled=True)]
    all_to_all x2, starting transfers between devices: 12 us -> 50.3 us  [local(): lax.all_to_all(labels, 'neuron', split_axis=0, concat_axis=0, tiled=True)]
    all_to_all x2, waiting for transfers between devices: 46.8 us -> 31.6 us  [local(): lax.all_to_all(outgoing, 'neuron', split_axis=0, concat_axis=0, tiled=True)]
    reshape x0 -> x2, other arithmetic: none -> 9.54 us  [local(): block_view = whole_acts.reshape(image_rows, all_blocks, block_width)]
    reshape x2 -> x0, local copies, waits for them, and re-layouts: 3.9 us -> none  [local(): block_view = whole_acts.reshape(image_rows, all_blocks, block_width)]
  transfers between devices with their start and end apart: 6 -> 34, of which waited for: 4 -> 30; matrix products, arithmetic and copies ran while one was open for 22% -> 16% of each run, Pallas kernels for 0% -> 0%
where the time goes in v1:
time: 362 us; the launch traced here: 359 us
  waiting for transfers between devices  230 us (64%)
  starting transfers between devices  66.2 us (18%)
  local copies, waits for them, and re-layouts  36.2 us (10%)
  other arithmetic  18.3 us (5%)
  matrix products  7.83 us (2%)
    ppermute x30, waiting for transfers between devices, local(): lax.ppermute(ring[-1], 'neuron', [(dev, (dev + 1) % 16) for dev in range(...  199 us
    all_to_all x2, starting transfers between devices, local(): lax.all_to_all(labels, 'neuron', split_axis=0, concat_axis=0, tiled=True)  50.3 us
    all_to_all x2, waiting for transfers between devices, local(): lax.all_to_all(outgoing, 'neuron', split_axis=0, concat_axis=0, tiled=True)  31.6 us
    scatter x2, local copies, waits for them, and re-layouts, local(): outgoing = jnp.zeros((devices * capacity, image_rows, block_width), jnp.f...  26.8 us
    all_to_all x2, starting transfers between devices, local(): lax.all_to_all(outgoing, 'neuron', split_axis=0, concat_axis=0, tiled=True)  12.8 us
    reshape x2, other arithmetic, local(): block_view = whole_acts.reshape(image_rows, all_blocks, block_width)  9.54 us
  transfers between devices with their start and end apart: 34, of which 30 were waited for; matrix products, arithmetic and copies ran while one was open for 16% of the time, Pallas kernels for 0%

profile of v1, /device:TPU:8, one launch (start us, length us, event | category | flops | bytes accessed | tf_op | source)
XLA Modules:
  0.0 359.3 jit_solution(17907441330698140460)
XLA Ops:
  0.0 1.5 collective-permute-start
  1.5 5.8 %collective-permute-done = bf16[16,4096]{1,0:T(8,128)(2,1)S(1)} collective-permute-done((bf16[16,4096]{1,0:T(8,128)(2,1)}, bf16[16,4096]{1,0:T(8,128)(2,1)S(1)}, u32[]{:S(2)}, u32[]{:S(2)}) %collective-permute-start) | collective-permute-done | bytes 131104 | tf_op jit(solution)/shard_map/ppermute | solution.py:24
  7.3 6.8 %collective-permute-done.1 = bf16[16,4096]{1,0:T(8,128)(2,1)S(1)} collective-permute-done((bf16[16,4096]{1,0:T(8,128)(2,1)S(1)}, bf16[16,4096]{1,0:T(8,128)(2,1)S(1)}, u32[]{:S(2)}, u32[]{:S(2)}) %collective-permute-start.1) | collective-permute-done | bytes 131104 | tf_op jit(solution)/shard_map/ppermute | solution.py:24
  14.0 6.8 %collective-permute-done.2 = bf16[16,4096]{1,0:T(8,128)(2,1)S(1)} collective-permute-done((bf16[16,4096]{1,0:T(8,128)(2,1)S(1)}, bf16[16,4096]{1,0:T(8,128)(2,1)S(1)}, u32[]{:S(2)}, u32[]{:S(2)}) %collective-permute-start.2) | collective-permute-done | bytes 131104 | tf_op jit(solution)/shard_map/ppermute | solution.py:24
  20.8 6.8 %collective-permute-done.3 = bf16[16,4096]{1,0:T(8,128)(2,1)S(1)} collective-permute-done((bf16[16,4096]{1,0:T(8,128)(2,1)S(1)}, bf16[16,4096]{1,0:T(8,128)(2,1)S(1)}, u32[]{:S(2)}, u32[]{:S(2)}) %collective-permute-start.3) | collective-permute-done | bytes 131104 | tf_op jit(solution)/shard_map/ppermute | solution.py:24
  27.6 8.0 %collective-permute-done.4 = bf16[16,4096]{1,0:T(8,128)(2,1)S(1)} collective-permute-done((bf16[16,4096]{1,0:T(8,128)(2,1)S(1)}, bf16[16,4096]{1,0:T(8,128)(2,1)S(1)}, u32[]{:S(2)}, u32[]{:S(2)}) %collective-permute-start.4) | collective-permute-done | bytes 131104 | tf_op jit(solution)/shard_map/ppermute | solution.py:24
  35.6 7.3 %collective-permute-done.5 = bf16[16,4096]{1,0:T(8,128)(2,1)S(1)} collective-permute-done((bf16[16,4096]{1,0:T(8,128)(2,1)S(1)}, bf16[16,4096]{1,0:T(8,128)(2,1)S(1)}, u32[]{:S(2)}, u32[]{:S(2)}) %collective-permute-start.5) | collective-permute-done | bytes 131104 | tf_op jit(solution)/shard_map/ppermute | solution.py:24
  42.9 6.8 %collective-permute-done.6 = bf16[16,4096]{1,0:T(8,128)(2,1)S(1)} collective-permute-done((bf16[16,4096]{1,0:T(8,128)(2,1)S(1)}, bf16[16,4096]{1,0:T(8,128)(2,1)S(1)}, u32[]{:S(2)}, u32[]{:S(2)}) %collective-permute-start.6) | collective-permute-done | bytes 131104 | tf_op jit(solution)/shard_map/ppermute | solution.py:24
  49.7 6.8 %collective-permute-done.7 = bf16[16,4096]{1,0:T(8,128)(2,1)S(1)} collective-permute-done((bf16[16,4096]{1,0:T(8,128)(2,1)S(1)}, bf16[16,4096]{1,0:T(8,128)(2,1)S(1)}, u32[]{:S(2)}, u32[]{:S(2)}) %collective-permute-start.7) | collective-permute-done | bytes 131104 | tf_op jit(solution)/shard_map/ppermute | solution.py:24
  56.5 0.7 fusion.41
  57.1 6.1 %collective-permute-done.8 = bf16[16,4096]{1,0:T(8,128)(2,1)S(1)} collective-permute-done((bf16[16,4096]{1,0:T(8,128)(2,1)S(1)}, bf16[16,4096]{1,0:T(8,128)(2,1)S(1)}, u32[]{:S(2)}, u32[]{:S(2)}) %collective-permute-start.8) | collective-permute-done | bytes 131104 | tf_op jit(solution)/shard_map/ppermute | solution.py:24
  63.2 0.7 fusion.40
  63.9 7.3 %collective-permute-done.9 = bf16[16,4096]{1,0:T(8,128)(2,1)S(1)} collective-permute-done((bf16[16,4096]{1,0:T(8,128)(2,1)S(1)}, bf16[16,4096]{1,0:T(8,128)(2,1)S(1)}, u32[]{:S(2)}, u32[]{:S(2)}) %collective-permute-start.9) | collective-permute-done | bytes 131104 | tf_op jit(solution)/shard_map/ppermute | solution.py:24
  71.2 0.7 and_select_fusion.4
  71.9 8.0 %collective-permute-done.10 = bf16[16,4096]{1,0:T(8,128)(2,1)S(1)} collective-permute-done((bf16[16,4096]{1,0:T(8,128)(2,1)S(1)}, bf16[16,4096]{1,0:T(8,128)(2,1)S(1)}, u32[]{:S(2)}, u32[]{:S(2)}) %collective-permute-start.10) | collective-permute-done | bytes 131104 | tf_op jit(solution)/shard_map/ppermute | solution.py:24
  79.9 1.4 fusion.51
  81.3 0.6 iota_compare_fusion.3
  82.0 6.0 %collective-permute-done.11 = bf16[16,4096]{1,0:T(8,128)(2,1)S(1)} collective-permute-done((bf16[16,4096]{1,0:T(8,128)(2,1)S(1)}, bf16[16,4096]{1,0:T(8,128)(2,1)S(1)}, u32[]{:S(2)}, u32[]{:S(2)}) %collective-permute-start.11) | collective-permute-done | bytes 131104 | tf_op jit(solution)/shard_map/ppermute | solution.py:24
  88.0 0.7 iota_compare_fusion.4
  88.9 7.7 %collective-permute-done.12 = bf16[16,4096]{1,0:T(8,128)(2,1)S(1)} collective-permute-done((bf16[16,4096]{1,0:T(8,128)(2,1)S(1)}, bf16[16,4096]{1,0:T(8,128)(2,1)S(1)}, u32[]{:S(2)}, u32[]{:S(2)}) %collective-permute-start.12) | collective-permute-done | bytes 131104 | tf_op jit(solution)/shard_map/ppermute | solution.py:24
  96.6 2.0 fusion.43
  98.6 1.0 scatter_custom_fusion.1
  99.6 0.7 all_to_all.20
  100.3 25.0 %all-to-all-start.1 = ((f32[16,8,1]{1,2,0:T(1,128)}), f32[16,8,1]{1,2,0:T(1,128)S(1)}, u32[]{:S(2)}, u32[]{:S(2)}) async-start(f32[16,8,1]{1,2,0:T(1,128)} %bitcast.13), calls=%async_computation.1 | async-start | bytes 16384 | tf_op jit(solution)/shard_map/all_to_all | solution.py:61
  125.3 1.5 collective-permute-start.14
  126.8 0.7 compare_and_fusion
  127.5 4.6 %collective-permute-done.14 = bf16[16,4096]{1,0:T(8,128)(2,1)S(1)} collective-permute-done((bf16[16,4096]{1,0:T(8,128)(2,1)S(1)}, bf16[16,4096]{1,0:T(8,128)(2,1)S(1)}, u32[]{:S(2)}, u32[]{:S(2)}) %collective-permute-start.14) | collective-permute-done | bytes 131104 | tf_op jit(solution)/shard_map/ppermute | solution.py:24
  132.4 4.8 %copy_bitcast_fusion.1 = bf16[16,512,128]{2,0,1:T(8,128)(2,1)S(1)} fusion(s32[]{:T(128)S(6)} %select_n.135, bf16[16,65536]{1,0:T(8,128)(2,1)S(1)} %constant_dynamic-update-slice_fusion), kind=kLoop, calls=%fused_computation.21 | loop fusion | flops 4194304 | bytes 4194308 | tf_op jit(solution)/shard_map/reshape | solution.py:31
  137.2 0.7 gather_fusion
  137.9 3.2 fusion.10
  141.1 1.1 broadcast.306.clone
  142.2 13.5 %scatter_fusion = f32[128,16,128]{2,1,0:T(8,128)} fusion(f32[128,16,128]{2,1,0:T(8,128)} %broadcast.306.clone, s32[128]{0:T(128)S(1)} %get-tuple-element.19, f32[128,16,128]{2,1,0:T(8,128)S(1)} %fusion.10), kind=kCustom, calls=%fused_computation.4 | custom fusion | bytes 3146240 | tf_op jit(solution)/shard_map/scatter | solution.py:52
  155.7 5.5 %all-to-all-start.2 = ((f32[128,16,128]{2,1,0:T(8,128)}), f32[128,16,128]{2,1,0:T(8,128)S(1)}, u32[]{:S(2)}, u32[]{:S(2)}) async-start(f32[128,16,128]{2,1,0:T(8,128)} %scatter_fusion), calls=%async_computation.2 | async-start | bytes 2097152 | tf_op jit(solution)/shard_map/all_to_all | solution.py:60
  161.2 0.6 broadcast.381
  161.7 0.6 reduce.6
  162.5 16.7 %all-to-all-done.2 = f32[128,16,128]{2,1,0:T(8,128)S(1)} async-done(((f32[128,16,128]{2,1,0:T(8,128)}), f32[128,16,128]{2,1,0:T(8,128)S(1)}, u32[]{:S(2)}, u32[]{:S(2)}) %all-to-all-start.2) | async-done | bytes 1048608 | tf_op jit(solution)/shard_map/all_to_all | solution.py:60
  179.2 0.7 fusion.18
  180.2 8.1 %collective-permute-done.15 = bf16[16,4096]{1,0:T(8,128)(2,1)S(1)} collective-permute-done((bf16[16,4096]{1,0:T(8,128)(2,1)S(1)}, bf16[16,4096]{1,0:T(8,128)(2,1)S(1)}, u32[]{:S(2)}, u32[]{:S(2)}) %collective-permute-start.15) | collective-permute-done | bytes 131104 | tf_op jit(solution)/shard_map/ppermute | solution.py:24
  188.3 7.3 %collective-permute-done.16 = bf16[16,4096]{1,0:T(8,128)(2,1)S(1)} collective-permute-done((bf16[16,4096]{1,0:T(8,128)(2,1)S(1)}, bf16[16,4096]{1,0:T(8,128)(2,1)S(1)}, u32[]{:S(2)}, u32[]{:S(2)}) %collective-permute-start.16) | collective-permute-done | bytes 131104 | tf_op jit(solution)/shard_map/ppermute | solution.py:24
  195.6 6.8 %collective-permute-done.17 = bf16[16,4096]{1,0:T(8,128)(2,1)S(1)} collective-permute-done((bf16[16,4096]{1,0:T(8,128)(2,1)S(1)}, bf16[16,4096]{1,0:T(8,128)(2,1)S(1)}, u32[]{:S(2)}, u32[]{:S(2)}) %collective-permute-start.17) | collective-permute-done | bytes 131104 | tf_op jit(solution)/shard_map/ppermute | solution.py:24
  202.4 6.8 %collective-permute-done.18 = bf16[16,4096]{1,0:T(8,128)(2,1)S(1)} collective-permute-done((bf16[16,4096]{1,0:T(8,128)(2,1)S(1)}, bf16[16,4096]{1,0:T(8,128)(2,1)S(1)}, u32[]{:S(2)}, u32[]{:S(2)}) %collective-permute-start.18) | collective-permute-done | bytes 131104 | tf_op jit(solution)/shard_map/ppermute | solution.py:24
  209.1 6.8 %collective-permute-done.19 = bf16[16,4096]{1,0:T(8,128)(2,1)S(1)} collective-permute-done((bf16[16,4096]{1,0:T(8,128)(2,1)S(1)}, bf16[16,4096]{1,0:T(8,128)(2,1)S(1)}, u32[]{:S(2)}, u32[]{:S(2)}) %collective-permute-start.19) | collective-permute-done | bytes 131104 | tf_op jit(solution)/shard_map/ppermute | solution.py:24
  215.9 7.4 %collective-permute-done.20 = bf16[16,4096]{1,0:T(8,128)(2,1)S(1)} collective-permute-done((bf16[16,4096]{1,0:T(8,128)(2,1)S(1)}, bf16[16,4096]{1,0:T(8,128)(2,1)S(1)}, u32[]{:S(2)}, u32[]{:S(2)}) %collective-permute-start.20) | collective-permute-done | bytes 131104 | tf_op jit(solution)/shard_map/ppermute | solution.py:24
  223.3 6.8 %collective-permute-done.21 = bf16[16,4096]{1,0:T(8,128)(2,1)S(1)} collective-permute-done((bf16[16,4096]{1,0:T(8,128)(2,1)S(1)}, bf16[16,4096]{1,0:T(8,128)(2,1)S(1)}, u32[]{:S(2)}, u32[]{:S(2)}) %collective-permute-start.21) | collective-permute-done | bytes 131104 | tf_op jit(solution)/shard_map/ppermute | solution.py:24
  230.1 7.1 %collective-permute-done.22 = bf16[16,4096]{1,0:T(8,128)(2,1)S(1)} collective-permute-done((bf16[16,4096]{1,0:T(8,128)(2,1)S(1)}, bf16[16,4096]{1,0:T(8,128)(2,1)S(1)}, u32[]{:S(2)}, u32[]{:S(2)}) %collective-permute-start.22) | collective-permute-done | bytes 131104 | tf_op jit(solution)/shard_map/ppermute | solution.py:24
  237.2 7.0 %collective-permute-done.23 = bf16[16,4096]{1,0:T(8,128)(2,1)S(1)} collective-permute-done((bf16[16,4096]{1,0:T(8,128)(2,1)S(1)}, bf16[16,4096]{1,0:T(8,128)(2,1)S(1)}, u32[]{:S(2)}, u32[]{:S(2)}) %collective-permute-start.23) | collective-permute-done | bytes 131104 | tf_op jit(solution)/shard_map/ppermute | solution.py:24
  244.2 6.8 %collective-permute-done.24 = bf16[16,4096]{1,0:T(8,128)(2,1)S(1)} collective-permute-done((bf16[16,4096]{1,0:T(8,128)(2,1)S(1)}, bf16[16,4096]{1,0:T(8,128)(2,1)S(1)}, u32[]{:S(2)}, u32[]{:S(2)}) %collective-permute-start.24) | collective-permute-done | bytes 131104 | tf_op jit(solution)/shard_map/ppermute | solution.py:24
  250.9 7.2 %collective-permute-done.25 = bf16[16,4096]{1,0:T(8,128)(2,1)S(1)} collective-permute-done((bf16[16,4096]{1,0:T(8,128)(2,1)S(1)}, bf16[16,4096]{1,0:T(8,128)(2,1)S(1)}, u32[]{:S(2)}, u32[]{:S(2)}) %collective-permute-start.25) | collective-permute-done | bytes 131104 | tf_op jit(solution)/shard_map/ppermute | solution.py:24
  258.1 8.6 %collective-permute-done.26 = bf16[16,4096]{1,0:T(8,128)(2,1)S(1)} collective-permute-done((bf16[16,4096]{1,0:T(8,128)(2,1)S(1)}, bf16[16,4096]{1,0:T(8,128)(2,1)S(1)}, u32[]{:S(2)}, u32[]{:S(2)}) %collective-permute-start.26) | collective-permute-done | bytes 131104 | tf_op jit(solution)/shard_map/ppermute | solution.py:24
  266.7 8.7 %collective-permute-done.27 = bf16[16,4096]{1,0:T(8,128)(2,1)S(1)} collective-permute-done((bf16[16,4096]{1,0:T(8,128)(2,1)S(1)}, bf16[16,4096]{1,0:T(8,128)(2,1)S(1)}, u32[]{:S(2)}, u32[]{:S(2)}) %collective-permute-start.27) | collective-permute-done | bytes 131104 | tf_op jit(solution)/shard_map/ppermute | solution.py:24
  275.4 8.9 %collective-permute-done.28 = bf16[16,4096]{1,0:T(8,128)(2,1)S(1)} collective-permute-done((bf16[16,4096]{1,0:T(8,128)(2,1)S(1)}, bf16[16,4096]{1,0:T(8,128)(2,1)S(1)}, u32[]{:S(2)}, u32[]{:S(2)}) %collective-permute-start.28) | collective-permute-done | bytes 131104 | tf_op jit(solution)/shard_map/ppermute | solution.py:24
  284.2 1.0 scatter_custom_fusion
  285.2 0.7 all_to_all.18
  285.9 25.3 %all-to-all-start = ((f32[16,8,1]{1,2,0:T(1,128)}), f32[16,8,1]{1,2,0:T(1,128)S(1)}, u32[]{:S(2)}, u32[]{:S(2)}) async-start(f32[16,8,1]{1,2,0:T(1,128)} %bitcast.5), calls=%async_computation | async-start | bytes 16384 | tf_op jit(solution)/shard_map/all_to_all | solution.py:61
  311.7 4.8 %copy_bitcast_fusion = bf16[16,512,128]{2,0,1:T(8,128)(2,1)S(1)} fusion(s32[]{:T(128)S(6)} %select_n.135, bf16[16,65536]{1,0:T(8,128)(2,1)S(1)} %constant_dynamic-update-slice_fusion.16), kind=kLoop, calls=%fused_computation.20 | loop fusion | flops 4194304 | bytes 4194308 | tf_op jit(solution)/shard_map/reshape | solution.py:31
  316.4 0.7 gather_fusion.1
  317.1 3.2 fusion.13
  320.3 1.1 broadcast.306
  321.4 13.3 %scatter_fusion.1 = f32[128,16,128]{2,1,0:T(8,128)} fusion(f32[128,16,128]{2,1,0:T(8,128)} %broadcast.306, s32[128]{0:T(128)S(1)} %get-tuple-element.20, f32[128,16,128]{2,1,0:T(8,128)S(1)} %fusion.13), kind=kCustom, calls=%fused_computation.5 | custom fusion | bytes 3146240 | tf_op jit(solution)/shard_map/scatter | solution.py:52
  334.8 7.3 %all-to-all-start.3 = ((f32[128,16,128]{2,1,0:T(8,128)}), f32[128,16,128]{2,1,0:T(8,128)S(1)}, u32[]{:S(2)}, u32[]{:S(2)}) async-start(f32[128,16,128]{2,1,0:T(8,128)} %scatter_fusion.1), calls=%async_computation.3 | async-start | bytes 2097152 | tf_op jit(solution)/shard_map/all_to_all | solution.py:60
  342.1 0.6 reduce.7
  342.8 14.9 %all-to-all-done.3 = f32[128,16,128]{2,1,0:T(8,128)S(1)} async-done(((f32[128,16,128]{2,1,0:T(8,128)}), f32[128,16,128]{2,1,0:T(8,128)S(1)}, u32[]{:S(2)}, u32[]{:S(2)}) %all-to-all-start.3) | async-done | bytes 1048608 | tf_op jit(solution)/shard_map/all_to_all | solution.py:60
  357.8 0.7 fusion.16
  358.5 0.8 fusion.27
  (75 shorter events, 1.2 us)
Async XLA Ops:
  0.0 132.4 %copy-start = (bf16[16,4096]{1,0:T(8,128)(2,1)S(1)}, bf16[16,4096]{1,0:T(8,128)(2,1)}, u32[]{:S(2)}) copy-start(bf16[16,4096]{1,0:T(8,128)(2,1)} %param.9) | copy-start | bytes 393220
  0.0 7.2 %collective-permute-start = (bf16[16,4096]{1,0:T(8,128)(2,1)}, bf16[16,4096]{1,0:T(8,128)(2,1)S(1)}, u32[]{:S(2)}, u32[]{:S(2)}) collective-permute-start(bf16[16,4096]{1,0:T(8,128)(2,1)} %param.9), channel_id=1, source_target_pairs={{0,1},{1,2},{2,3},{3,4},{4,5},{5,6},{6,7},{7,8},{8,9},{9,10},{10,1... | collective-permute-start | bytes 393224 | tf_op jit(solution)/shard_map/ppermute | solution.py:24
  7.2 6.8 %collective-permute-start.1 = (bf16[16,4096]{1,0:T(8,128)(2,1)S(1)}, bf16[16,4096]{1,0:T(8,128)(2,1)S(1)}, u32[]{:S(2)}, u32[]{:S(2)}) collective-permute-start(bf16[16,4096]{1,0:T(8,128)(2,1)S(1)} %collective-permute-done), channel_id=1, source_target_pairs={{0,1},{1,2},{2,3},{3,4},{4,5},{5,6},{6,7},{7,8},{8,9},{9,10},{10,1... | collective-permute-start | bytes 393224 | tf_op jit(solution)/shard_map/ppermute | solution.py:24
  14.0 6.8 %collective-permute-start.2 = (bf16[16,4096]{1,0:T(8,128)(2,1)S(1)}, bf16[16,4096]{1,0:T(8,128)(2,1)S(1)}, u32[]{:S(2)}, u32[]{:S(2)}) collective-permute-start(bf16[16,4096]{1,0:T(8,128)(2,1)S(1)} %collective-permute-done.1), channel_id=1, source_target_pairs={{0,1},{1,2},{2,3},{3,4},{4,5},{5,6},{6,7},{7,8},{8,9},{9,10},{10,1... | collective-permute-start | bytes 393224 | tf_op jit(solution)/shard_map/ppermute | solution.py:24
  20.8 6.8 %collective-permute-start.3 = (bf16[16,4096]{1,0:T(8,128)(2,1)S(1)}, bf16[16,4096]{1,0:T(8,128)(2,1)S(1)}, u32[]{:S(2)}, u32[]{:S(2)}) collective-permute-start(bf16[16,4096]{1,0:T(8,128)(2,1)S(1)} %collective-permute-done.2), channel_id=1, source_target_pairs={{0,1},{1,2},{2,3},{3,4},{4,5},{5,6},{6,7},{7,8},{8,9},{9,10},{10,1... | collective-permute-start | bytes 393224 | tf_op jit(solution)/shard_map/ppermute | solution.py:24
  27.6 8.0 %collective-permute-start.4 = (bf16[16,4096]{1,0:T(8,128)(2,1)S(1)}, bf16[16,4096]{1,0:T(8,128)(2,1)S(1)}, u32[]{:S(2)}, u32[]{:S(2)}) collective-permute-start(bf16[16,4096]{1,0:T(8,128)(2,1)S(1)} %collective-permute-done.3), channel_id=1, source_target_pairs={{0,1},{1,2},{2,3},{3,4},{4,5},{5,6},{6,7},{7,8},{8,9},{9,10},{10,1... | collective-permute-start | bytes 393224 | tf_op jit(solution)/shard_map/ppermute | solution.py:24
  35.6 7.3 %collective-permute-start.5 = (bf16[16,4096]{1,0:T(8,128)(2,1)S(1)}, bf16[16,4096]{1,0:T(8,128)(2,1)S(1)}, u32[]{:S(2)}, u32[]{:S(2)}) collective-permute-start(bf16[16,4096]{1,0:T(8,128)(2,1)S(1)} %collective-permute-done.4), channel_id=1, source_target_pairs={{0,1},{1,2},{2,3},{3,4},{4,5},{5,6},{6,7},{7,8},{8,9},{9,10},{10,1... | collective-permute-start | bytes 393224 | tf_op jit(solution)/shard_map/ppermute | solution.py:24
  42.9 6.8 %collective-permute-start.6 = (bf16[16,4096]{1,0:T(8,128)(2,1)S(1)}, bf16[16,4096]{1,0:T(8,128)(2,1)S(1)}, u32[]{:S(2)}, u32[]{:S(2)}) collective-permute-start(bf16[16,4096]{1,0:T(8,128)(2,1)S(1)} %collective-permute-done.5), channel_id=1, source_target_pairs={{0,1},{1,2},{2,3},{3,4},{4,5},{5,6},{6,7},{7,8},{8,9},{9,10},{10,1... | collective-permute-start | bytes 393224 | tf_op jit(solution)/shard_map/ppermute | solution.py:24
  49.7 6.8 %collective-permute-start.7 = (bf16[16,4096]{1,0:T(8,128)(2,1)S(1)}, bf16[16,4096]{1,0:T(8,128)(2,1)S(1)}, u32[]{:S(2)}, u32[]{:S(2)}) collective-permute-start(bf16[16,4096]{1,0:T(8,128)(2,1)S(1)} %collective-permute-done.6), channel_id=1, source_target_pairs={{0,1},{1,2},{2,3},{3,4},{4,5},{5,6},{6,7},{7,8},{8,9},{9,10},{10,1... | collective-permute-start | bytes 393224 | tf_op jit(solution)/shard_map/ppermute | solution.py:24
  56.5 6.8 %collective-permute-start.8 = (bf16[16,4096]{1,0:T(8,128)(2,1)S(1)}, bf16[16,4096]{1,0:T(8,128)(2,1)S(1)}, u32[]{:S(2)}, u32[]{:S(2)}) collective-permute-start(bf16[16,4096]{1,0:T(8,128)(2,1)S(1)} %collective-permute-done.7), channel_id=1, source_target_pairs={{0,1},{1,2},{2,3},{3,4},{4,5},{5,6},{6,7},{7,8},{8,9},{9,10},{10,1... | collective-permute-start | bytes 393224 | tf_op jit(solution)/shard_map/ppermute | solution.py:24
  63.2 8.0 %collective-permute-start.9 = (bf16[16,4096]{1,0:T(8,128)(2,1)S(1)}, bf16[16,4096]{1,0:T(8,128)(2,1)S(1)}, u32[]{:S(2)}, u32[]{:S(2)}) collective-permute-start(bf16[16,4096]{1,0:T(8,128)(2,1)S(1)} %collective-permute-done.8), channel_id=1, source_target_pairs={{0,1},{1,2},{2,3},{3,4},{4,5},{5,6},{6,7},{7,8},{8,9},{9,10},{10,1... | collective-permute-start | bytes 393224 | tf_op jit(solution)/shard_map/ppermute | solution.py:24
  71.2 8.7 %collective-permute-start.10 = (bf16[16,4096]{1,0:T(8,128)(2,1)S(1)}, bf16[16,4096]{1,0:T(8,128)(2,1)S(1)}, u32[]{:S(2)}, u32[]{:S(2)}) collective-permute-start(bf16[16,4096]{1,0:T(8,128)(2,1)S(1)} %collective-permute-done.9), channel_id=1, source_target_pairs={{0,1},{1,2},{2,3},{3,4},{4,5},{5,6},{6,7},{7,8},{8,9},{9,10},{10,1... | collective-permute-start | bytes 393224 | tf_op jit(solution)/shard_map/ppermute | solution.py:24
  79.9 8.1 %collective-permute-start.11 = (bf16[16,4096]{1,0:T(8,128)(2,1)S(1)}, bf16[16,4096]{1,0:T(8,128)(2,1)S(1)}, u32[]{:S(2)}, u32[]{:S(2)}) collective-permute-start(bf16[16,4096]{1,0:T(8,128)(2,1)S(1)} %collective-permute-done.10), channel_id=1, source_target_pairs={{0,1},{1,2},{2,3},{3,4},{4,5},{5,6},{6,7},{7,8},{8,9},{9,10},{10,1... | collective-permute-start | bytes 393224 | tf_op jit(solution)/shard_map/ppermute | solution.py:24
  88.0 8.6 %collective-permute-start.12 = (bf16[16,4096]{1,0:T(8,128)(2,1)S(1)}, bf16[16,4096]{1,0:T(8,128)(2,1)S(1)}, u32[]{:S(2)}, u32[]{:S(2)}) collective-permute-start(bf16[16,4096]{1,0:T(8,128)(2,1)S(1)} %collective-permute-done.11), channel_id=1, source_target_pairs={{0,1},{1,2},{2,3},{3,4},{4,5},{5,6},{6,7},{7,8},{8,9},{9,10},{10,1... | collective-permute-start | bytes 393224 | tf_op jit(solution)/shard_map/ppermute | solution.py:24
  96.6 28.7 %collective-permute-start.13 = (bf16[16,4096]{1,0:T(8,128)(2,1)S(1)}, bf16[16,4096]{1,0:T(8,128)(2,1)S(1)}, u32[]{:S(2)}, u32[]{:S(2)}) collective-permute-start(bf16[16,4096]{1,0:T(8,128)(2,1)S(1)} %collective-permute-done.12), channel_id=1, source_target_pairs={{0,1},{1,2},{2,3},{3,4},{4,5},{5,6},{6,7},{7,8},{8,9},{9,10},{10,1... | collective-permute-start | bytes 393224 | tf_op jit(solution)/shard_map/ppermute | solution.py:24
  100.3 55.4 %all-to-all-start.1 = ((f32[16,8,1]{1,2,0:T(1,128)}), f32[16,8,1]{1,2,0:T(1,128)S(1)}, u32[]{:S(2)}, u32[]{:S(2)}) async-start(f32[16,8,1]{1,2,0:T(1,128)} %bitcast.13), calls=%async_computation.1 | async-start | bytes 16384 | tf_op jit(solution)/shard_map/all_to_all | solution.py:61
  125.3 6.8 %collective-permute-start.14 = (bf16[16,4096]{1,0:T(8,128)(2,1)S(1)}, bf16[16,4096]{1,0:T(8,128)(2,1)S(1)}, u32[]{:S(2)}, u32[]{:S(2)}) collective-permute-start(bf16[16,4096]{1,0:T(8,128)(2,1)S(1)} %collective-permute-done.13), channel_id=1, source_target_pairs={{0,1},{1,2},{2,3},{3,4},{4,5},{5,6},{6,7},{7,8},{8,9},{9,10},{10,1... | collective-permute-start | bytes 393224 | tf_op jit(solution)/shard_map/ppermute | solution.py:24
  142.2 18.9 %copy-start.1 = (f32[2,4096]{1,0:T(2,128)S(1)}, f32[2,4096]{1,0:T(2,128)}, u32[]{:S(2)}) copy-start(f32[2,4096]{1,0:T(2,128)} %param.13) | copy-start | bytes 98308
  155.7 23.5 %all-to-all-start.2 = ((f32[128,16,128]{2,1,0:T(8,128)}), f32[128,16,128]{2,1,0:T(8,128)S(1)}, u32[]{:S(2)}, u32[]{:S(2)}) async-start(f32[128,16,128]{2,1,0:T(8,128)} %scatter_fusion), calls=%async_computation.2 | async-start | bytes 2097152 | tf_op jit(solution)/shard_map/all_to_all | solution.py:60
  180.1 8.2 %collective-permute-start.15 = (bf16[16,4096]{1,0:T(8,128)(2,1)S(1)}, bf16[16,4096]{1,0:T(8,128)(2,1)S(1)}, u32[]{:S(2)}, u32[]{:S(2)}) collective-permute-start(bf16[16,4096]{1,0:T(8,128)(2,1)S(1)} %fusion.29), channel_id=1, source_target_pairs={{0,1},{1,2},{2,3},{3,4},{4,5},{5,6},{6,7},{7,8},{8,9},{9,10},{10,1... | collective-permute-start | bytes 393224 | tf_op jit(solution)/shard_map/ppermute | solution.py:24
  188.3 7.3 %collective-permute-start.16 = (bf16[16,4096]{1,0:T(8,128)(2,1)S(1)}, bf16[16,4096]{1,0:T(8,128)(2,1)S(1)}, u32[]{:S(2)}, u32[]{:S(2)}) collective-permute-start(bf16[16,4096]{1,0:T(8,128)(2,1)S(1)} %collective-permute-done.15), channel_id=1, source_target_pairs={{0,1},{1,2},{2,3},{3,4},{4,5},{5,6},{6,7},{7,8},{8,9},{9,10},{10,1... | collective-permute-start | bytes 393224 | tf_op jit(solution)/shard_map/ppermute | solution.py:24
  195.6 6.8 %collective-permute-start.17 = (bf16[16,4096]{1,0:T(8,128)(2,1)S(1)}, bf16[16,4096]{1,0:T(8,128)(2,1)S(1)}, u32[]{:S(2)}, u32[]{:S(2)}) collective-permute-start(bf16[16,4096]{1,0:T(8,128)(2,1)S(1)} %collective-permute-done.16), channel_id=1, source_target_pairs={{0,1},{1,2},{2,3},{3,4},{4,5},{5,6},{6,7},{7,8},{8,9},{9,10},{10,1... | collective-permute-start | bytes 393224 | tf_op jit(solution)/shard_map/ppermute | solution.py:24
  202.4 6.8 %collective-permute-start.18 = (bf16[16,4096]{1,0:T(8,128)(2,1)S(1)}, bf16[16,4096]{1,0:T(8,128)(2,1)S(1)}, u32[]{:S(2)}, u32[]{:S(2)}) collective-permute-start(bf16[16,4096]{1,0:T(8,128)(2,1)S(1)} %collective-permute-done.17), channel_id=1, source_target_pairs={{0,1},{1,2},{2,3},{3,4},{4,5},{5,6},{6,7},{7,8},{8,9},{9,10},{10,1... | collective-permute-start | bytes 393224 | tf_op jit(solution)/shard_map/ppermute | solution.py:24
  209.1 6.8 %collective-permute-start.19 = (bf16[16,4096]{1,0:T(8,128)(2,1)S(1)}, bf16[16,4096]{1,0:T(8,128)(2,1)S(1)}, u32[]{:S(2)}, u32[]{:S(2)}) collective-permute-start(bf16[16,4096]{1,0:T(8,128)(2,1)S(1)} %collective-permute-done.18), channel_id=1, source_target_pairs={{0,1},{1,2},{2,3},{3,4},{4,5},{5,6},{6,7},{7,8},{8,9},{9,10},{10,1... | collective-permute-start | bytes 393224 | tf_op jit(solution)/shard_map/ppermute | solution.py:24
  215.9 7.4 %collective-permute-start.20 = (bf16[16,4096]{1,0:T(8,128)(2,1)S(1)}, bf16[16,4096]{1,0:T(8,128)(2,1)S(1)}, u32[]{:S(2)}, u32[]{:S(2)}) collective-permute-start(bf16[16,4096]{1,0:T(8,128)(2,1)S(1)} %collective-permute-done.19), channel_id=1, source_target_pairs={{0,1},{1,2},{2,3},{3,4},{4,5},{5,6},{6,7},{7,8},{8,9},{9,10},{10,1... | collective-permute-start | bytes 393224 | tf_op jit(solution)/shard_map/ppermute | solution.py:24
  223.3 6.8 %collective-permute-start.21 = (bf16[16,4096]{1,0:T(8,128)(2,1)S(1)}, bf16[16,4096]{1,0:T(8,128)(2,1)S(1)}, u32[]{:S(2)}, u32[]{:S(2)}) collective-permute-start(bf16[16,4096]{1,0:T(8,128)(2,1)S(1)} %collective-permute-done.20), channel_id=1, source_target_pairs={{0,1},{1,2},{2,3},{3,4},{4,5},{5,6},{6,7},{7,8},{8,9},{9,10},{10,1... | collective-permute-start | bytes 393224 | tf_op jit(solution)/shard_map/ppermute | solution.py:24
  230.1 7.1 %collective-permute-start.22 = (bf16[16,4096]{1,0:T(8,128)(2,1)S(1)}, bf16[16,4096]{1,0:T(8,128)(2,1)S(1)}, u32[]{:S(2)}, u32[]{:S(2)}) collective-permute-start(bf16[16,4096]{1,0:T(8,128)(2,1)S(1)} %collective-permute-done.21), channel_id=1, source_target_pairs={{0,1},{1,2},{2,3},{3,4},{4,5},{5,6},{6,7},{7,8},{8,9},{9,10},{10,1... | collective-permute-start | bytes 393224 | tf_op jit(solution)/shard_map/ppermute | solution.py:24
  237.2 7.0 %collective-permute-start.23 = (bf16[16,4096]{1,0:T(8,128)(2,1)S(1)}, bf16[16,4096]{1,0:T(8,128)(2,1)S(1)}, u32[]{:S(2)}, u32[]{:S(2)}) collective-permute-start(bf16[16,4096]{1,0:T(8,128)(2,1)S(1)} %collective-permute-done.22), channel_id=1, source_target_pairs={{0,1},{1,2},{2,3},{3,4},{4,5},{5,6},{6,7},{7,8},{8,9},{9,10},{10,1... | collective-permute-start | bytes 393224 | tf_op jit(solution)/shard_map/ppermute | solution.py:24
  244.2 6.8 %collective-permute-start.24 = (bf16[16,4096]{1,0:T(8,128)(2,1)S(1)}, bf16[16,4096]{1,0:T(8,128)(2,1)S(1)}, u32[]{:S(2)}, u32[]{:S(2)}) collective-permute-start(bf16[16,4096]{1,0:T(8,128)(2,1)S(1)} %collective-permute-done.23), channel_id=1, source_target_pairs={{0,1},{1,2},{2,3},{3,4},{4,5},{5,6},{6,7},{7,8},{8,9},{9,10},{10,1... | collective-permute-start | bytes 393224 | tf_op jit(solution)/shard_map/ppermute | solution.py:24
  250.9 7.2 %collective-permute-start.25 = (bf16[16,4096]{1,0:T(8,128)(2,1)S(1)}, bf16[16,4096]{1,0:T(8,128)(2,1)S(1)}, u32[]{:S(2)}, u32[]{:S(2)}) collective-permute-start(bf16[16,4096]{1,0:T(8,128)(2,1)S(1)} %collective-permute-done.24), channel_id=1, source_target_pairs={{0,1},{1,2},{2,3},{3,4},{4,5},{5,6},{6,7},{7,8},{8,9},{9,10},{10,1... | collective-permute-start | bytes 393224 | tf_op jit(solution)/shard_map/ppermute | solution.py:24
  258.1 8.6 %collective-permute-start.26 = (bf16[16,4096]{1,0:T(8,128)(2,1)S(1)}, bf16[16,4096]{1,0:T(8,128)(2,1)S(1)}, u32[]{:S(2)}, u32[]{:S(2)}) collective-permute-start(bf16[16,4096]{1,0:T(8,128)(2,1)S(1)} %collective-permute-done.25), channel_id=1, source_target_pairs={{0,1},{1,2},{2,3},{3,4},{4,5},{5,6},{6,7},{7,8},{8,9},{9,10},{10,1... | collective-permute-start | bytes 393224 | tf_op jit(solution)/shard_map/ppermute | solution.py:24
  266.7 8.7 %collective-permute-start.27 = (bf16[16,4096]{1,0:T(8,128)(2,1)S(1)}, bf16[16,4096]{1,0:T(8,128)(2,1)S(1)}, u32[]{:S(2)}, u32[]{:S(2)}) collective-permute-start(bf16[16,4096]{1,0:T(8,128)(2,1)S(1)} %collective-permute-done.26), channel_id=1, source_target_pairs={{0,1},{1,2},{2,3},{3,4},{4,5},{5,6},{6,7},{7,8},{8,9},{9,10},{10,1... | collective-permute-start | bytes 393224 | tf_op jit(solution)/shard_map/ppermute | solution.py:24
  275.4 8.9 %collective-permute-start.28 = (bf16[16,4096]{1,0:T(8,128)(2,1)S(1)}, bf16[16,4096]{1,0:T(8,128)(2,1)S(1)}, u32[]{:S(2)}, u32[]{:S(2)}) collective-permute-start(bf16[16,4096]{1,0:T(8,128)(2,1)S(1)} %collective-permute-done.27), channel_id=1, source_target_pairs={{0,1},{1,2},{2,3},{3,4},{4,5},{5,6},{6,7},{7,8},{8,9},{9,10},{10,1... | collective-permute-start | bytes 393224 | tf_op jit(solution)/shard_map/ppermute | solution.py:24
  284.2 26.9 %collective-permute-start.29 = (bf16[16,4096]{1,0:T(8,128)(2,1)S(1)}, bf16[16,4096]{1,0:T(8,128)(2,1)S(1)}, u32[]{:S(2)}, u32[]{:S(2)}) collective-permute-start(bf16[16,4096]{1,0:T(8,128)(2,1)S(1)} %collective-permute-done.28), channel_id=1, source_target_pairs={{0,1},{1,2},{2,3},{3,4},{4,5},{5,6},{6,7},{7,8},{8,9},{9,10},{10,1... | collective-permute-start | bytes 393224 | tf_op jit(solution)/shard_map/ppermute | solution.py:24
  285.9 48.8 %all-to-all-start = ((f32[16,8,1]{1,2,0:T(1,128)}), f32[16,8,1]{1,2,0:T(1,128)S(1)}, u32[]{:S(2)}, u32[]{:S(2)}) async-start(f32[16,8,1]{1,2,0:T(1,128)} %bitcast.5), calls=%async_computation | async-start | bytes 16384 | tf_op jit(solution)/shard_map/all_to_all | solution.py:61
  334.8 23.0 %all-to-all-start.3 = ((f32[128,16,128]{2,1,0:T(8,128)}), f32[128,16,128]{2,1,0:T(8,128)S(1)}, u32[]{:S(2)}, u32[]{:S(2)}) async-start(f32[128,16,128]{2,1,0:T(8,128)} %scatter_fusion.1), calls=%async_computation.3 | async-start | bytes 2097152 | tf_op jit(solution)/shard_map/all_to_all | solution.py:60
